TPU v7x, 32 devices: a whole 2x2x4 slice. The times are simulated.
32 devices in a mesh: gz: 8 (over z, y), gy: 4 (over x, core).
Axes of the slice: x: 2, y: 2, z: 4, core: 2. Of those that a mesh axis runs over, the one named last changes fastest.
Arguments:
- charges: float32 [64, 64, 1024], P('gz', 'gy'), may hold values from -6 to 6
- kernel: float32 [64, 64, 64], P('gz', 'gy'), may hold values from -0.01171875 to 0.01171875
Outputs:
- fine_potential: float32 [128, 128, 2048], P('gz', 'gy')
All inputs are finite; a program needn't handle non-finite values.
Results may differ from a plain program's by a relative error of at most 0.000098.
Values sent between devices are 32-bit elements; how exact they have to be, the bound alone decides.
A program may use at most 128 MiB of HBM per device.

v0:
```python
import math

import jax
import jax.numpy as jnp
import numpy as np
from jax import lax
from jax.sharding import PartitionSpec as P

AXES = ("gz", "gy")


def angle(first, second, count):
    return 2.0 * np.pi / count * ((first * second) % count)


def x_table(count, replicas, devices):
    half = replicas // 2
    columns = count * half // devices
    device, part, column, x, side, pair = np.ix_(
        *(np.arange(s) for s in (devices, 2, columns, count, 2, half))
    )
    flat = device * columns + column
    theta = angle(flat // half, x, count)
    value = np.where(part == side, np.cos(theta), np.where(part == 0, np.sin(theta), -np.sin(theta)))
    value = value * (flat % half == pair)
    return value.reshape(devices * 2 * columns, count, replicas)


def x_kernel_table(count, replicas, devices):
    half = replicas // 2
    columns = count * half // devices
    lines = max(1, columns // half)
    device, part, line, x = np.ix_(*(np.arange(s) for s in (devices, 2, lines, count)))
    theta = angle(device * columns // half + line, x, count)
    value = np.where(part == 0, np.cos(theta), -np.sin(theta))
    return value.reshape(devices * 2 * lines, count)


def y_table(count, planes, rows):
    part, block, plane, row, new_plane, new_part, freq = np.ix_(
        *(np.arange(s) for s in (2, count // rows, planes, rows, planes, 2, count))
    )
    theta = angle(block * rows + row, freq, count)
    value = np.where(
        part == new_part, np.cos(theta), np.where(new_part == 0, np.sin(theta), -np.sin(theta))
    )
    value = value * (plane == new_plane)
    return value.reshape(2 * count * planes, planes * 2 * count)


def z_table(count, planes, columns, lines, group, wave):
    blocks = count // planes
    low, high, column, z_low, z_high, line = np.ix_(
        *(np.arange(s) for s in (planes, blocks, columns, planes, blocks, lines))
    )
    theta = angle(high * planes + low, z_high * planes + z_low, count)
    value = wave(theta) * (column // group == line)
    return value.reshape(count * columns, count * lines)


def refined(values, axis):
    before = np.roll(values, 1, axis)
    after = np.roll(values, -1, axis)
    after_two = np.roll(values, -2, axis)
    middle = (9.0 * (values + after) - (before + after_two)) / 16.0
    stacked = np.stack([values, middle], axis=axis + 1)
    shape = list(values.shape)
    shape[axis] = 2 * shape[axis]
    return stacked.reshape(shape)


def const(values):
    return jnp.asarray(np.asarray(values, np.float32))


def dot(left, right, dims=((1,), (0,))):
    return lax.dot_general(
        left, right, (dims, ((), ())), precision=lax.Precision.HIGH,
        preferred_element_type=jnp.float32,
    )


def extended(block, axis, dim):
    size = lax.axis_size(axis)
    forward = [(i, (i + 1) % size) for i in range(size)]
    backward = [(target, source) for source, target in forward]
    low = lax.ppermute(lax.slice_in_dim(block, block.shape[dim] - 1, None, axis=dim), axis, forward)
    high = lax.ppermute(lax.slice_in_dim(block, 0, 2, axis=dim), axis, backward)
    return jnp.concatenate([low, block, high], axis=dim)


def refine_rim(haloed, axis, count):
    centre = lax.slice_in_dim(haloed, 1, 1 + count, axis=axis)
    before = lax.slice_in_dim(haloed, 0, count, axis=axis)
    after = lax.slice_in_dim(haloed, 2, 2 + count, axis=axis)
    after_two = lax.slice_in_dim(haloed, 3, 3 + count, axis=axis)
    middle = (9.0 * (centre + after) - (before + after_two)) / 16.0
    stacked = jnp.stack([centre, middle], axis=axis + 1)
    shape = list(centre.shape)
    shape[axis] = 2 * count
    return stacked.reshape(shape)


def per_device(charges, kernel):
    planes, rows, count = kernel.shape
    replicas = charges.shape[2] // count
    half = replicas // 2
    blocks_z, blocks_y = lax.axis_size("gz"), lax.axis_size("gy")
    devices = blocks_z * blocks_y
    place = planes * rows
    columns = count * half // devices
    lines = max(1, columns // half)
    table_x = x_table(count, replicas, devices)
    table_y = const(y_table(count, planes, rows))
    cos_z = const(z_table(count, planes, columns, columns, 1, np.cos))
    sin_z = const(z_table(count, planes, columns, columns, 1, np.sin))
    cos_k = const(z_table(count, planes, columns, lines, half, np.cos) / count**3)
    sin_k = const(z_table(count, planes, columns, lines, half, np.sin) / count**3)

    sent = dot(const(table_x.reshape(-1, count * replicas)), charges.reshape(place, -1), ((1,), (1,)))
    sent_k = dot(const(x_kernel_table(count, replicas, devices)), kernel.reshape(place, count), ((1,), (1,)))
    both = jnp.concatenate(
        [sent.reshape(devices, 2 * columns, place), sent_k.reshape(devices, 2 * lines, place)], axis=1
    )
    both = lax.all_to_all(both, AXES, split_axis=0, concat_axis=0, tiled=True)

    def by_y(block, width):
        block = block.reshape(blocks_z, blocks_y, 2, width, place).transpose(0, 3, 2, 1, 4)
        block = dot(block.reshape(blocks_z * width, 2 * blocks_y * place), table_y)
        block = block.reshape(blocks_z * width, planes, 2 * count).transpose(1, 0, 2)
        return block.reshape(count * width, 2 * count)

    def swap(values):
        return jnp.concatenate([values[:, count:], values[:, :count]], axis=1)

    sign = jnp.where(lax.broadcasted_iota(jnp.int32, (1, 2 * count), 1) < count, 1.0, -1.0)
    data = by_y(both[:, : 2 * columns], columns)
    green = by_y(both[:, 2 * columns :], lines)
    data = dot(cos_z, data) + sign * swap(dot(sin_z, data))
    green = dot(cos_k, green) + sign * swap(dot(sin_k, green))
    real, imag = green[:, :count], green[:, count:]
    data = data * jnp.concatenate([real, real], axis=1) + swap(data) * jnp.concatenate([-imag, imag], axis=1)
    data = dot(cos_z, data) - sign * swap(dot(sin_z, data))
    data = data.reshape(planes, blocks_z * columns, 2 * count).transpose(1, 0, 2)
    data = dot(data.reshape(blocks_z * columns, planes * 2 * count), table_y, ((1,), (1,)))
    data = data.reshape(blocks_z, columns, 2, blocks_y, place).transpose(0, 3, 2, 1, 4)
    data = lax.all_to_all(
        data.reshape(devices, 2 * columns, place), AXES, split_axis=0, concat_axis=0, tiled=True
    )
    fine_x = const(refined(table_x, 1).reshape(-1, 2 * count * replicas))
    result = dot(data.reshape(devices * 2 * columns, place), fine_x, ((0,), (0,)))
    result = result.reshape(planes, rows, 2 * count * replicas)
    result = extended(extended(result, "gz", 0), "gy", 1)
    result = refine_rim(result, 0, planes)
    return refine_rim(result, 1, rows)


def solution(mesh):
    placed = (P("gz", "gy", None), P("gz", "gy", None))
    return jax.shard_map(
        per_device, mesh=mesh, in_specs=placed, out_specs=P("gz", "gy", None), check_vma=False
    )
```

profile of v0, /device:TPU:1, one launch (start us, length us, event | category | flops | bytes accessed | tf_op | source)
XLA Modules:
  0.0 114.4 jit_solution(8732151330638290631)
XLA Ops:
  0.0 1.1 fusion.21
  1.2 4.0 %fusion.20 = f32[32,32,128]{2,1,0:T(8,128)S(1)} fusion(f32[32,32,1024]{2,1,0:T(8,128)} %constant.41, f32[128,1024,1]{1,0,2:T(8,128)S(1)} %bitcast.70), kind=kOutput, calls=%fused_computation.46 | convolution fusion | flops 805306368 | bytes 5242880 | tf_op jit(solution)/shard_map/dot_general | solution.py:77
  5.2 0.9 pad_maximum_fusion.3
  6.1 7.3 %all-to-all-start = ((f32[32,36,128]{2,1,0:T(8,128)}), f32[32,36,128]{2,1,0:T(8,128)S(1)}, u32[]{:S(2)}, u32[]{:S(2)}) async-start(f32[32,36,128]{2,1,0:T(8,128)} %pad_maximum_fusion.3), calls=%async_computation | async-start | bytes 1310720 | tf_op jit(solution)/shard_map/all_to_all | solution.py:125
  13.4 17.6 %all-to-all-done = f32[32,36,128]{2,1,0:T(8,128)S(1)} async-done(((f32[32,36,128]{2,1,0:T(8,128)}), f32[32,36,128]{2,1,0:T(8,128)S(1)}, u32[]{:S(2)}, u32[]{:S(2)}) %all-to-all-start) | async-done | bytes 589856 | tf_op jit(solution)/shard_map/all_to_all | solution.py:125
  31.7 4.5 %fusion.22 = f32[128,8,128]{2,0,1:T(8,128)S(1)} fusion(f32[128,1024,1]{1,0,2:T(8,128)S(1)} %reshape.92, f32[8,128,1024]{2,1,0:T(8,128)} %constant.44), kind=kOutput, calls=%fused_computation.48 | convolution fusion | flops 805306368 | bytes 5242880 | tf_op jit(solution)/shard_map/dot_general | solution.py:77
  36.3 1.9 %fusion.23 = f32[16,8,128]{2,0,1:T(8,128)S(1)} fusion(f32[16,1024,1]{1,0,2:T(8,128)S(1)} %reshape.93, f32[8,128,1024]{2,1,0:T(8,128)S(1)} %copy-done.2), kind=kOutput, calls=%fused_computation.49 | convolution fusion | flops 100663296 | bytes 4325376 | tf_op jit(solution)/shard_map/dot_general | solution.py:77
  38.7 2.4 %fusion.10 = f32[1024,128]{0,1:T(8,128)S(1)} fusion(f32[1024,1024]{1,0:T(8,128)S(1)} %copy-done.4, f32[128,8,128]{2,0,1:T(8,128)S(1)} %fusion.22), kind=kOutput, calls=%fused_computation.30 | convolution fusion | flops 805306368 | bytes 5242880 | tf_op jit(solution)/shard_map/dot_general | solution.py:77
  41.2 0.4 convolution_add_fusion.1
  41.6 2.4 %convolution_add_fusion = f32[1024,128]{0,1:T(8,128)S(1)} fusion(f32[1024,1024]{1,0:T(8,128)S(1)} %copy-done.6, f32[1024,64]{0,1:T(8,128)S(1)} %get-tuple-element.19, f32[1024,64]{0,1:T(8,128)S(1)} %get-tuple-element.18, f32[128,8,128]{2,0,1:T(8,128)S(1)} %fusion.22, f32[128]{0:T(128)S(1)} %compare_select_fusion), kind=kOutput, calls=%fused_computation.16 | convolution fusion | flops 805699584 | bytes 5767680 | tf_op jit(solution)/shard_map/dot_general | solution.py:77
  44.4 1.9 %copy-done.3 = f32[1024,1024]{1,0:T(8,128)S(1)} copy-done((f32[1024,1024]{1,0:T(8,128)S(1)}, f32[1024,1024]{1,0:T(8,128)}, u32[]{:S(2)}) %copy-start.3) | copy-done | bytes 4194328
  46.3 2.2 %fusion.24 = f32[1024,128]{0,1:T(8,128)S(1)} fusion(f32[1024,1024]{1,0:T(8,128)S(1)} %copy-done.3, f32[1024,128]{0,1:T(8,128)S(1)} %fusion.8), kind=kOutput, calls=%fused_computation.50 | convolution fusion | flops 805306368 | bytes 5242880 | tf_op jit(solution)/shard_map/dot_general | solution.py:77
  48.5 2.2 %fusion.7 = f32[16,8,8,128]{3,1,2,0:T(8,128)S(1)} fusion(f32[1024,1024]{1,0:T(8,128)S(1)} %copy-done.5, f32[1024,128]{0,1:T(8,128)S(1)} %fusion.8, f32[1024,64]{0,1:T(8,128)S(1)} %get-tuple-element.10, f32[1024,64]{0,1:T(8,128)S(1)} %get-tuple-element.9, f32[128]{0:T(128)S(1)} %compare_select_fusion), kind=kOutput, calls=%fused_computation.17 | convolution fusion | flops 805699584 | bytes 5767680 | tf_op jit(solution)/shard_map/dot_general | solution.py:77
  50.8 0.5 copy.38
  51.4 4.4 %convolution_bitcast_fusion = f32[8,4,2,16,128]{4,3,1,2,0:T(8,128)S(1)} fusion(f32[2,4,128,1024,1]{3,2,1,0,4:T(8,128)} %constant.55, f32[8,16,1024,1,1]{2,1,0,3,4:T(8,128)S(1)} %reshape.94), kind=kOutput, calls=%fused_computation.18 | convolution fusion | flops 805306368 | bytes 5242880 | tf_op jit(solution)/shard_map/dot_general | solution.py:77
  55.9 18.6 %all_to_all.10 = f32[32,32,128]{2,1,0:T(8,128)S(1)} all-to-all(f32[32,32,128]{2,1,0:T(8,128)S(1)} %bitcast.75), channel_id=1, replica_groups=mesh['gz'=8,'gy'=4] {'gz','gy'}, dimensions={0} | all-to-all | bytes 1048576 | tf_op jit(solution)/shard_map/all_to_all | solution.py:147
  74.5 5.8 %fusion.25 = f32[128,2048]{1,0:T(8,128)S(1)} fusion(f32[1024,128]{1,0:T(8,128)S(1)} %bitcast.73, f32[1024,2048]{1,0:T(8,128)} %constant.37.clone), kind=kOutput, calls=%fused_computation.51 | convolution fusion | flops 1610612736 | bytes 9961472 | tf_op jit(solution)/shard_map/dot_general | solution.py:77
  80.5 1.6 %collective-permute-start.1 = (f32[2,16,2048]{2,0,1:T(2,128)S(1)}, f32[2,16,2048]{2,0,1:T(2,128)S(1)}, u32[]{:S(2)}, u32[]{:S(2)}) collective-permute-start(f32[2,16,2048]{2,0,1:T(2,128)S(1)} %copy.40), channel_id=1, source_target_pairs={{4,0},{8,4},{12,8},{16,12},{20,16},{24,20},{28,24},{0,28},{5,1},{9... | collective-permute-start | bytes 786440 | tf_op jit(solution)/shard_map/ppermute | solution.py:88
  82.2 0.6 copy.42
  82.8 8.0 %collective-permute-done = f32[1,16,2048]{2,1,0:T(8,128)S(1)} collective-permute-done((f32[1,16,2048]{2,1,0:T(8,128)S(1)}, f32[1,16,2048]{2,1,0:T(8,128)S(1)}, u32[]{:S(2)}, u32[]{:S(2)}) %collective-permute-start) | collective-permute-done | bytes 131104 | tf_op jit(solution)/shard_map/ppermute | solution.py:87
  91.0 1.2 %collective-permute-start.3 = (f32[11,2,2048]{2,0,1:T(8,128)S(1)}, f32[11,2,2048]{2,0,1:T(8,128)S(1)}, u32[]{:S(2)}, u32[]{:S(2)}) collective-permute-start(f32[11,2,2048]{2,0,1:T(8,128)S(1)} %pad_maximum_fusion.4), channel_id=1, source_target_pairs={{1,0},{2,1},{3,2},{0,3},{5,4},{6,5},{7,6},{4,7},{9,8},{10,9},{11,1... | collective-permute-start | bytes 540680 | tf_op jit(solution)/shard_map/ppermute | solution.py:88
  92.2 1.0 collective-permute-start.2
  93.3 3.3 %collective-permute-done.2 = f32[11,1,2048]{2,0,1:T(8,128)S(1)} collective-permute-done((f32[11,1,2048]{2,0,1:T(8,128)S(1)}, f32[11,1,2048]{2,0,1:T(8,128)S(1)}, u32[]{:S(2)}, u32[]{:S(2)}) %collective-permute-start.2) | collective-permute-done | bytes 90144 | tf_op jit(solution)/shard_map/ppermute | solution.py:87
  96.6 2.0 %collective-permute-done.3 = f32[11,2,2048]{2,0,1:T(8,128)S(1)} collective-permute-done((f32[11,2,2048]{2,0,1:T(8,128)S(1)}, f32[11,2,2048]{2,0,1:T(8,128)S(1)}, u32[]{:S(2)}, u32[]{:S(2)}) %collective-permute-start.3) | collective-permute-done | bytes 180256 | tf_op jit(solution)/shard_map/ppermute | solution.py:88
  99.1 0.4 slice_bitcast_fusion.1
  99.5 1.3 %copy.43 = f32[8,1,19,2048]{3,1,0,2:T(1,128)S(1)} copy(f32[8,1,19,2048]{3,0,2,1:T(8,128)S(1)} %get-tuple-element.7) | data formatting | bytes 2490368 | tf_op jit(solution)/shard_map/stack | solution.py:98
  100.8 0.9 stack.19
  101.7 3.7 %pad_maximum_fusion.2 = f32[8,2,19,2048]{3,1,0,2:T(2,128)} fusion(f32[8,1,19,2048]{3,1,0,2:T(1,128)S(1)} %stack.19, f32[8,1,19,2048]{3,1,0,2:T(1,128)S(1)} %copy.43), kind=kLoop, calls=%fused_computation.2 | loop fusion | flops 622592 | bytes 4980736 | tf_op jit(solution)/shard_map/stack | solution.py:98
  105.4 3.2 %reshape.76 = f32[16,19,2048]{2,0,1:T(8,128)S(1)} reshape(f32[8,2,19,2048]{3,1,0,2:T(2,128)} %pad_maximum_fusion.2) | data formatting | bytes 4980736 | tf_op jit(solution)/shard_map/reshape | solution.py:101
  108.7 0.5 slice_bitcast_fusion
  109.2 0.5 pad_maximum_fusion
  110.0 4.4 %copy.45 = f32[16,32,2048]{2,1,0:T(8,128)} copy(f32[16,32,2048]{2,0,1:T(8,128)S(1)} %bitcast.71) | data formatting | bytes 8388608 | tf_op jit(solution)/shard_map/reshape | solution.py:101
  (44 shorter events, 3.0 us)
Async XLA Ops:
  0.0 1.2 %copy-start = (f32[8,16,1024]{2,1,0:T(8,128)S(1)}, f32[8,16,1024]{2,1,0:T(8,128)}, u32[]{:S(2)}) copy-start(f32[8,16,1024]{2,1,0:T(8,128)} %param.10) | copy-start | bytes 1572868
  6.1 24.9 %all-to-all-start = ((f32[32,36,128]{2,1,0:T(8,128)}), f32[32,36,128]{2,1,0:T(8,128)S(1)}, u32[]{:S(2)}, u32[]{:S(2)}) async-start(f32[32,36,128]{2,1,0:T(8,128)} %pad_maximum_fusion.3), calls=%async_computation | async-start | bytes 1310720 | tf_op jit(solution)/shard_map/all_to_all | solution.py:125
  31.7 4.6 %copy-start.2 = (f32[8,128,1024]{2,1,0:T(8,128)S(1)}, f32[8,128,1024]{2,1,0:T(8,128)}, u32[]{:S(2)}) copy-start(f32[8,128,1024]{2,1,0:T(8,128)} %constant.44) | copy-start | bytes 12582916
  31.7 6.5 %copy-start.8 = (f32[1024,128]{1,0:T(8,128)S(1)}, f32[1024,128]{1,0:T(8,128)}, u32[]{:S(2)}) copy-start(f32[1024,128]{1,0:T(8,128)} %constant.53) | copy-start | bytes 1572868
  36.3 2.4 %copy-start.4 = (f32[1024,1024]{1,0:T(8,128)S(1)}, f32[1024,1024]{1,0:T(8,128)}, u32[]{:S(2)}) copy-start(f32[1024,1024]{1,0:T(8,128)} %constant.47) | copy-start | bytes 12582916
  38.7 2.5 %copy-start.7 = (f32[1024,128]{1,0:T(8,128)S(1)}, f32[1024,128]{1,0:T(8,128)}, u32[]{:S(2)}) copy-start(f32[1024,128]{1,0:T(8,128)} %constant.50) | copy-start | bytes 1572868
  38.7 2.9 %copy-start.6 = (f32[1024,1024]{1,0:T(8,128)S(1)}, f32[1024,1024]{1,0:T(8,128)}, u32[]{:S(2)}) copy-start(f32[1024,1024]{1,0:T(8,128)} %constant.40) | copy-start | bytes 12582916
  44.1 2.2 %copy-start.3 = (f32[1024,1024]{1,0:T(8,128)S(1)}, f32[1024,1024]{1,0:T(8,128)}, u32[]{:S(2)}) copy-start(f32[1024,1024]{1,0:T(8,128)} %constant.32.clone) | copy-start | bytes 12582916
  46.2 2.3 %copy-start.5 = (f32[1024,1024]{1,0:T(8,128)S(1)}, f32[1024,1024]{1,0:T(8,128)}, u32[]{:S(2)}) copy-start(f32[1024,1024]{1,0:T(8,128)} %constant.31.clone) | copy-start | bytes 12582916
  80.5 10.4 %collective-permute-start.1 = (f32[2,16,2048]{2,0,1:T(2,128)S(1)}, f32[2,16,2048]{2,0,1:T(2,128)S(1)}, u32[]{:S(2)}, u32[]{:S(2)}) collective-permute-start(f32[2,16,2048]{2,0,1:T(2,128)S(1)} %copy.40), channel_id=1, source_target_pairs={{4,0},{8,4},{12,8},{16,12},{20,16},{24,20},{28,24},{0,28},{5,1},{9... | collective-permute-start | bytes 786440 | tf_op jit(solution)/shard_map/ppermute | solution.py:88
  82.1 8.7 %collective-permute-start = (f32[1,16,2048]{2,1,0:T(8,128)S(1)}, f32[1,16,2048]{2,1,0:T(8,128)S(1)}, u32[]{:S(2)}, u32[]{:S(2)}) collective-permute-start(f32[1,16,2048]{2,1,0:T(8,128)S(1)} %slice_bitcast_fusion.2), channel_id=1, source_target_pairs={{0,4},{4,8},{8,12},{12,16},{16,20},{20,24},{24,28},{28,0},{1,5},{5... | collective-permute-start | bytes 393224 | tf_op jit(solution)/shard_map/ppermute | solution.py:87
  91.0 7.7 %collective-permute-start.3 = (f32[11,2,2048]{2,0,1:T(8,128)S(1)}, f32[11,2,2048]{2,0,1:T(8,128)S(1)}, u32[]{:S(2)}, u32[]{:S(2)}) collective-permute-start(f32[11,2,2048]{2,0,1:T(8,128)S(1)} %pad_maximum_fusion.4), channel_id=1, source_target_pairs={{1,0},{2,1},{3,2},{0,3},{5,4},{6,5},{7,6},{4,7},{9,8},{10,9},{11,1... | collective-permute-start | bytes 540680 | tf_op jit(solution)/shard_map/ppermute | solution.py:88
  92.2 4.4 %collective-permute-start.2 = (f32[11,1,2048]{2,0,1:T(8,128)S(1)}, f32[11,1,2048]{2,0,1:T(8,128)S(1)}, u32[]{:S(2)}, u32[]{:S(2)}) collective-permute-start(f32[11,1,2048]{2,0,1:T(8,128)S(1)} %pad_maximum_fusion.6), channel_id=1, source_target_pairs={{0,1},{1,2},{2,3},{3,0},{4,5},{5,6},{6,7},{7,4},{8,9},{9,10},{10,1... | collective-permute-start | bytes 270344 | tf_op jit(solution)/shard_map/ppermute | solution.py:87
  110.0 4.5 %copy-start.1 = (f32[8,16,1024]{2,1,0:T(8,128)S(1)}, f32[8,16,1024]{2,1,0:T(8,128)}, u32[]{:S(2)}) copy-start(f32[8,16,1024]{2,1,0:T(8,128)} %param.10) | copy-start | bytes 1572868
where the time goes:
time: 115 us; the launch traced here: 114 us
  matrix products  31.8 us (28%)
  waiting for transfers between devices  31 us (27%)
  blocking collectives  18.6 us (16%)
  local copies, waits for them, and re-layouts  14.6 us (13%)
  starting transfers between devices  11.1 us (10%)
  other arithmetic  6.83 us (6%)
    dot_general x12, matrix products, dot(): lax.dot_general(left, right, (dims, ((), ())), precision=lax.Precision.HI...  31.8 us
    all_to_all x1, blocking collectives, per_device(): lax.all_to_all(data.reshape(devices, 2 * columns, place), AXES, split_axi...  18.6 us
    all_to_all x1, waiting for transfers between devices, per_device(): both = lax.all_to_all(both, AXES, split_axis=0, concat_axis=0, tiled=True)  17.6 us
    ppermute x2, waiting for transfers between devices, extended(): lax.ppermute(lax.slice_in_dim(block, block.shape[dim] - 1, None, axis=dim...  11.3 us
    reshape x2, local copies, waits for them, and re-layouts, refine_rim(): return stacked.reshape(shape)  7.69 us
    all_to_all x1, starting transfers between devices, per_device(): both = lax.all_to_all(both, AXES, split_axis=0, concat_axis=0, tiled=True)  7.26 us
    another operation x4, other arithmetic, refine_rim(): stacked = jnp.stack([centre, middle], axis=axis + 1)  5.18 us
    ppermute x2, starting transfers between devices, extended(): high = lax.ppermute(lax.slice_in_dim(block, 0, 2, axis=dim), axis, backward)  2.79 us
  transfers between devices with their start and end apart: 5, of which 4 were waited for; matrix products, arithmetic and copies ran while one was open for 1% of the time, Pallas kernels for 0%

commit v1 on v0

--- a/solution.py
+++ b/solution.py
@@ -1,9 +1,11 @@
-import math
+import functools
 
 import jax
 import jax.numpy as jnp
 import numpy as np
 from jax import lax
+from jax.experimental import pallas as pl
+from jax.experimental.pallas import tpu as pltpu
 from jax.sharding import PartitionSpec as P
 
 AXES = ("gz", "gy")
@@ -101,7 +103,7 @@
     return stacked.reshape(shape)
 
 
-def per_device(charges, kernel):
+def plain(charges, kernel):
     planes, rows, count = kernel.shape
     replicas = charges.shape[2] // count
     half = replicas // 2
@@ -155,6 +157,242 @@
     return refine_rim(result, 1, rows)
 
 
+LANES = 128
+MESH = pl.DeviceIdType.MESH
+
+
+def table(values):
+    high = np.asarray(values, np.float32).astype(jnp.bfloat16)
+    low = (np.asarray(values, np.float64) - high.astype(np.float64)).astype(jnp.bfloat16)
+    return [jnp.asarray(high), jnp.asarray(low)]
+
+
+def split(values):
+    high = values.astype(jnp.bfloat16)
+    return high, (values - high.astype(jnp.float32)).astype(jnp.bfloat16)
+
+
+def mul(left, right, dims=((1,), (0,))):
+    return lax.dot_general(left, right, (dims, ((), ())), preferred_element_type=jnp.float32)
+
+
+def mul3(left, right, dims=((1,), (0,))):
+    (a, b), (c, d) = left, right
+    return mul(a, d, dims) + mul(b, c, dims) + mul(a, c, dims)
+
+
+def call(body, out_shape, *operands):
+    return pl.pallas_call(
+        body,
+        out_shape=jax.ShapeDtypeStruct(out_shape, jnp.float32),
+        in_specs=[pl.BlockSpec(memory_space=pltpu.VMEM)] * len(operands),
+        out_specs=pl.BlockSpec(memory_space=pltpu.VMEM),
+        compiler_params=pltpu.CompilerParams(vmem_limit_bytes=60 * 1024 * 1024),
+    )(*operands)
+
+
+def exchange_kernel(blocks_z, blocks_y, x_ref, o_ref, send_sem, recv_sem, own_sem):
+    devices = blocks_z * blocks_y
+    me = lax.axis_index("gz") * blocks_y + lax.axis_index("gy")
+
+    def partner(step):
+        other = lax.rem(me + step, devices)
+        return other, (other // blocks_y, lax.rem(other, blocks_y))
+
+    barrier = pltpu.get_barrier_semaphore()
+    for step in range(1, devices):
+        pl.semaphore_signal(barrier, inc=1, device_id=partner(step)[1], device_id_type=MESH)
+    own = pltpu.make_async_copy(x_ref.at[me], o_ref.at[me], own_sem)
+    own.start()
+    pl.semaphore_wait(barrier, devices - 1)
+    copies = []
+    for step in range(1, devices):
+        other, place = partner(step)
+        copy = pltpu.make_async_remote_copy(
+            src_ref=x_ref.at[other], dst_ref=o_ref.at[me],
+            send_sem=send_sem.at[step], recv_sem=recv_sem.at[step],
+            device_id=place, device_id_type=MESH,
+        )
+        copy.start()
+        copies.append(copy)
+    for copy in copies:
+        copy.wait()
+    own.wait()
+
+
+def exchange(blocks, blocks_z, blocks_y, number):
+    devices = blocks_z * blocks_y
+    return pl.pallas_call(
+        functools.partial(exchange_kernel, blocks_z, blocks_y),
+        out_shape=jax.ShapeDtypeStruct(blocks.shape, blocks.dtype),
+        in_specs=[pl.BlockSpec(memory_space=pltpu.VMEM)],
+        out_specs=pl.BlockSpec(memory_space=pltpu.VMEM),
+        scratch_shapes=[
+            pltpu.SemaphoreType.DMA((devices,)),
+            pltpu.SemaphoreType.DMA((devices,)),
+            pltpu.SemaphoreType.DMA,
+        ],
+        compiler_params=pltpu.CompilerParams(collective_id=number, has_side_effects=True),
+    )(blocks)
+
+
+def first_kernel(width, q_ref, k_ref, wh, wl, kh, kl, o_ref):
+    devices = o_ref.shape[0]
+    dims = ((1,), (1,))
+    sent = mul3((wh[...], wl[...]), split(q_ref[...]), dims)
+    o_ref[:, :width, :] = sent.reshape(devices, width, LANES)
+    sent = mul3((kh[...], kl[...]), split(k_ref[...]), dims)
+    o_ref[:, width:, :] = sent.reshape(devices, 8, LANES)
+
+
+def middle_kernel(columns, count, x_ref, yh, yl, ch, cl, sh, sl, ah, al, bh, bl, o_ref):
+    blocks_z, blocks_y = o_ref.shape[0], o_ref.shape[1]
+    planes = count // blocks_z
+    table_y = (yh[...], yl[...])
+    cos_z, sin_z = (ch[...], cl[...]), (sh[...], sl[...])
+    lane = lax.broadcasted_iota(jnp.int32, (1, LANES), 1)
+    sign = jnp.where(lane < count, 1.0, -1.0)
+
+    def swap(values):
+        return pltpu.roll(values, count, 1)
+
+    def lines_first(values):
+        return jnp.concatenate([values[:, p * LANES : (p + 1) * LANES] for p in range(planes)], axis=0)
+
+    data = jnp.concatenate(
+        [
+            x_ref[:, y, c * columns : (c + 1) * columns, :].reshape(blocks_z * columns, LANES)
+            for c in range(2)
+            for y in range(blocks_y)
+        ],
+        axis=1,
+    )
+    green = jnp.concatenate(
+        [x_ref[:, y, 2 * columns :, :].reshape(blocks_z * 8, LANES) for y in range(blocks_y)], axis=1
+    )
+    data = lines_first(mul3(split(data), table_y))
+    deep = blocks_y * LANES
+    green = lines_first(mul3(split(green), (yh[:deep, :], yl[:deep, :])))
+    data = split(data)
+    data = mul3(cos_z, data) + sign * swap(mul3(sin_z, data))
+    green = split(green)
+    green = mul3((ah[...], al[...]), green) - sign * swap(mul3((bh[...], bl[...]), green))
+    other = swap(green)
+    real = jnp.where(lane < count, green, other)
+    imag = jnp.where(lane < count, -other, green)
+    data = split(data * real + swap(data) * imag)
+    data = mul3(cos_z, data) - sign * swap(mul3(sin_z, data))
+    size = blocks_z * columns
+    data = jnp.concatenate([data[p * size : (p + 1) * size, :] for p in range(planes)], axis=1)
+    data = mul3(split(data), table_y, ((1,), (1,)))
+    for c in range(2):
+        for y in range(blocks_y):
+            start = (c * blocks_y + y) * LANES
+            o_ref[:, y, c * columns : (c + 1) * columns, :] = data[:, start : start + LANES].reshape(
+                blocks_z, columns, LANES
+            )
+
+
+def last_kernel(x_ref, wh, wl, o_ref):
+    turned = jnp.transpose(x_ref[...])
+    o_ref[...] = mul3(split(turned), (wh[...], wl[...]))
+
+
+def refine_kernel(x_ref, r_ref, t_ref, o_ref):
+    step = pl.program_id(0)
+    near = x_ref[pl.ds(step, 4)].reshape(4 * x_ref.shape[1], x_ref.shape[2])
+    high, low = split(near)
+    fine = mul(r_ref[...], low) + mul(r_ref[...], high)
+    high, low = split(fine)
+    blocks = fine.shape[1] // LANES
+    for b in range(blocks):
+        def window(values):
+            pieces = [(b + s) % blocks * LANES for s in (-1, 0, 1)]
+            return jnp.concatenate([values[:, p : p + LANES] for p in pieces], axis=1)
+
+        made = mul(window(low), t_ref[...]) + mul(window(high), t_ref[...])
+        o_ref[:, :, 2 * b * LANES : 2 * (b + 1) * LANES] = made.reshape(2, -1, 2 * LANES)
+
+
+def rim_table(count):
+    made = np.zeros((2 * count, count + 3))
+    for i in range(count):
+        made[2 * i, i + 1] = 1.0
+        made[2 * i + 1, i : i + 4] = np.array([-1.0, 9.0, 9.0, -1.0]) / 16.0
+    return made
+
+
+def refine(coarse, planes, rows, width, replicas):
+    haloed = extended(extended(coarse, "gz", 0), "gy", 1)
+    deep = -(-(rows + 3) // 8) * 8
+    haloed = jnp.pad(haloed, ((0, 0), (0, deep - rows - 3), (0, 0)))
+    along_y = np.pad(rim_table(rows), ((0, 0), (0, deep - rows - 3)))
+    both = jnp.asarray(np.kron(rim_table(1), along_y), jnp.bfloat16)
+    count = width // replicas
+    spread = refined(np.eye(width).reshape(width, count, replicas), 1).reshape(width, 2 * width)
+    spread = jnp.asarray(spread[: 3 * LANES, 2 * LANES : 4 * LANES], jnp.bfloat16)
+    return pl.pallas_call(
+        refine_kernel,
+        grid=(planes,),
+        out_shape=jax.ShapeDtypeStruct((2 * planes, 2 * rows, 2 * width), jnp.float32),
+        in_specs=[
+            pl.BlockSpec(haloed.shape, lambda i: (0, 0, 0)),
+            pl.BlockSpec(both.shape, lambda i: (0, 0)),
+            pl.BlockSpec(spread.shape, lambda i: (0, 0)),
+        ],
+        out_specs=pl.BlockSpec((2, 2 * rows, 2 * width), lambda i: (i, 0, 0)),
+    )(haloed, both, spread)
+
+
+def z_green_table(count, planes, columns, group, first, second):
+    lines = max(1, columns // group)
+    rows = []
+    for wave in (first, second):
+        made = z_table(count, planes, columns, lines, group, wave)
+        rows.append(made.reshape(count * columns, count, lines))
+    made = np.concatenate(rows, axis=2)
+    made = np.pad(made, ((0, 0), (0, 0), (0, 8 - 2 * lines)))
+    return made.reshape(count * columns, count * 8)
+
+
+def per_device(charges, kernel):
+    planes, rows, count = kernel.shape
+    width = charges.shape[2]
+    replicas = width // count
+    half = replicas // 2
+    blocks_z, blocks_y = lax.axis_size("gz"), lax.axis_size("gy")
+    devices = blocks_z * blocks_y
+    place = planes * rows
+    columns = count * half // devices
+    lines = max(1, columns // half)
+    fits = place == LANES and 2 * count == LANES and columns % 8 == 0 and 2 * lines <= 8
+    if not fits or LANES % replicas or width < 3 * LANES:
+        return plain(charges, kernel)
+    table_x = table(x_table(count, replicas, devices).reshape(-1, width))
+    lines_x = x_kernel_table(count, replicas, devices).reshape(devices, 2 * lines, count)
+    lines_x = table(np.pad(lines_x, ((0, 0), (0, 8 - 2 * lines), (0, 0))).reshape(devices * 8, count))
+    table_y = table(y_table(count, planes, rows))
+    cos_z = table(z_table(count, planes, columns, columns, 1, np.cos))
+    sin_z = table(z_table(count, planes, columns, columns, 1, np.sin))
+    scale = 1.0 / count**3
+    green_a = table(scale * z_green_table(count, planes, columns, half, np.cos, np.sin))
+    green_b = table(scale * z_green_table(count, planes, columns, half, lambda t: -np.sin(t), np.cos))
+
+    sent = call(
+        functools.partial(first_kernel, 2 * columns), (devices, 2 * columns + 8, LANES),
+        charges.reshape(place, width), kernel.reshape(place, count), *table_x, *lines_x,
+    )
+    held = exchange(sent, blocks_z, blocks_y, 0)
+    sent = call(
+        functools.partial(middle_kernel, columns, count), (blocks_z, blocks_y, 2 * columns, LANES),
+        held.reshape(blocks_z, blocks_y, 2 * columns + 8, LANES),
+        *table_y, *cos_z, *sin_z, *green_a, *green_b,
+    )
+    held = exchange(sent.reshape(devices, 2 * columns, LANES), blocks_z, blocks_y, 1)
+    coarse = call(last_kernel, (place, width), held.reshape(width, LANES), *table_x)
+    return refine(coarse.reshape(planes, rows, width), planes, rows, width, replicas)
+
+
 def solution(mesh):
     placed = (P("gz", "gy", None), P("gz", "gy", None))
     return jax.shard_map(

time: 115 us -> 98.6 us (0.86)
  Pallas kernels: 0 us -> 75.5 us
  matrix products: 31.8 us -> 0 us
  waiting for transfers between devices: 31 us -> 8.3 us
  blocking collectives: 18.6 us -> 0 us
  local copies, waits for them, and re-layouts: 14.6 us -> 1.83 us
  other arithmetic: 6.83 us -> 2.24 us
    pallas_call x0 -> x6, Pallas kernels: none -> 75.5 us  [the longest x2 39.5 us: exchange(): pl.pallas_call(functools.partial(exchange_kernel, blocks_z, blocks_y), ou...]
    dot_general x12 -> x0, matrix products: 31.8 us -> none  [dot(): lax.dot_general(left, right, (dims, ((), ())), precision=lax.Precision.HI...]
    all_to_all x1 -> x0, blocking collectives: 18.6 us -> none  [per_device(): lax.all_to_all(data.reshape(devices, 2 * columns, place), AXES, split_axi...]
    all_to_all x1 -> x0, waiting for transfers between devices: 17.6 us -> none  [per_device(): both = lax.all_to_all(both, AXES, split_axis=0, concat_axis=0, tiled=True)]
    reshape x5 -> x0, local copies, waits for them, and re-layouts: 8.54 us -> none  [the longest x2 7.69 us: refine_rim(): return stacked.reshape(shape)]
    all_to_all x1 -> x0, starting transfers between devices: 7.26 us -> none  [per_device(): both = lax.all_to_all(both, AXES, split_axis=0, concat_axis=0, tiled=True)]
    ppermute x2, starting transfers between devices: 2.79 us -> 8.83 us  [extended(): high = lax.ppermute(lax.slice_in_dim(block, 0, 2, axis=dim), axis, backward)]
    another operation x4 -> x0, other arithmetic: 5.18 us -> none  [refine_rim(): stacked = jnp.stack([centre, middle], axis=axis + 1)]
  transfers between devices with their start and end apart: 5 -> 4, of which waited for: 4 -> 3; matrix products, arithmetic and copies ran while one was open for 1% -> 1% of each run, Pallas kernels for 0% -> 0%
where the time goes in v1:
time: 98.6 us; the launch traced here: 98.2 us
  Pallas kernels  75.5 us (77%)
  starting transfers between devices  10.3 us (10%)
  waiting for transfers between devices  8.3 us (8%)
  other arithmetic  2.24 us (2%)
  local copies, waits for them, and re-layouts  1.83 us (2%)
    pallas_call x2, Pallas kernels, exchange(): pl.pallas_call(functools.partial(exchange_kernel, blocks_z, blocks_y), ou...  39.5 us
    pallas_call x3, Pallas kernels, call(): pl.pallas_call(body, out_shape=jax.ShapeDtypeStruct(out_shape, jnp.float3...  27.8 us
    ppermute x2, starting transfers between devices, extended(): high = lax.ppermute(lax.slice_in_dim(block, 0, 2, axis=dim), axis, backward)  8.83 us
    pallas_call x1, Pallas kernels, refine(): pl.pallas_call(refine_kernel, grid=(planes,), out_shape=jax.ShapeDtypeStr...  8.21 us
    ppermute x2, waiting for transfers between devices, extended(): lax.ppermute(lax.slice_in_dim(block, block.shape[dim] - 1, None, axis=dim...  6.95 us
    concatenate x2, other arithmetic, extended(): return jnp.concatenate([low, block, high], axis=dim)  2.2 us
  transfers between devices with their start and end apart: 4, of which 3 were waited for; matrix products, arithmetic and copies ran while one was open for 1% of the time, Pallas kernels for 0%

profile of v1, /device:TPU:1, one launch (start us, length us, event | category | flops | bytes accessed | tf_op | source)
XLA Modules:
  0.0 98.2 jit_solution(11071420142442607636)
XLA Ops:
  0.0 5.1 %shard_map.172.x_ref = f32[32,40,128]{2,1,0:T(8,128)} custom-call(f32[128,1024]{1,0:T(8,128)} %bitcast.15, f32[128,64]{1,0:T(8,128)} %bitcast.17, bf16[1024,1024]{1,0:T(8,128)(2,1)} %constant.35.clone.wh, bf16[1024,1024]{1,0:T(8,128)(2,1)} %constant.36.clone.wl, bf16[256,64]{1,0:T(8,128)(2,1)} %constant.37.clone.kh, bf16[256,64]{1,0:T(8,128)(2,1)} %constant.38.clone.kl), custom_call_target="tpu_custom_call" | custom-call | tf_op jit(solution)/shard_map/pallas_call | solution.py:185
  5.1 19.6 %shard_map.173 = f32[32,40,128]{2,1,0:T(8,128)} custom-call(f32[32,40,128]{2,1,0:T(8,128)} %shard_map.172.x_ref), custom_call_target="tpu_custom_call" | custom-call | tf_op jit(solution)/shard_map/pallas_call | solution.py:225
  24.7 18.5 %shard_map.174 = f32[8,4,32,128]{3,2,1,0:T(8,128)} custom-call(f32[8,4,40,128]{3,2,1,0:T(8,128)} %bitcast.12, bf16[1024,1024]{1,0:T(8,128)(2,1)} %constant.39.clone.yh, bf16[1024,1024]{1,0:T(8,128)(2,1)} %constant.40.clone.yl, bf16[1024,1024]{1,0:T(8,128)(2,1)} %constant.41.clone.ch, bf16[1024,1024]{1,0:T(8,128)(2,1)} %constant.42.clone.cl, ...), custom_call_target="tpu_custom_call" | custom-call | tf_op jit(solution)/shard_map/pallas_call | solution.py:185
  43.2 19.9 %shard_map.175 = f32[32,32,128]{2,1,0:T(8,128)} custom-call(f32[32,32,128]{2,1,0:T(8,128)} %bitcast.13), custom_call_target="tpu_custom_call" | custom-call | tf_op jit(solution)/shard_map/pallas_call | solution.py:225
  63.1 4.2 %shard_map.176 = f32[128,1024]{1,0:T(8,128)} custom-call(f32[1024,128]{1,0:T(8,128)} %bitcast.14, bf16[1024,1024]{1,0:T(8,128)(2,1)} %constant.35.clone.wh, bf16[1024,1024]{1,0:T(8,128)(2,1)} %constant.36.clone.wl), custom_call_target="tpu_custom_call" | custom-call | tf_op jit(solution)/shard_map/pallas_call | solution.py:185
  67.3 0.0 copy-start
  67.3 1.0 %slice.25 = f32[32,1024]{1,0:T(8,128)S(1)} slice(f32[128,1024]{1,0:T(8,128)} %shard_map.176), slice={[0:32], [0:1024]} | slice | bytes 262144 | tf_op jit(solution)/shard_map/slice | solution.py:90
  68.3 7.0 %collective-permute-start.1 = (f32[2,16,1024]{2,1,0:T(8,128)S(1)}, f32[2,16,1024]{2,1,0:T(8,128)S(1)}, u32[]{:S(2)}, u32[]{:S(2)}) collective-permute-start(f32[2,16,1024]{2,1,0:T(8,128)S(1)} %bitcast.16), channel_id=1, source_target_pairs={{4,0},{8,4},{12,8},{16,12},{20,16},{24,20},{28,24},{0,28},{5,1},{9... | collective-permute-start | bytes 393224 | tf_op jit(solution)/shard_map/ppermute | solution.py:90
  75.3 0.8 slice_bitcast_fusion
  76.1 0.0 collective-permute-start
  76.1 5.8 %collective-permute-done = f32[1,16,1024]{2,1,0:T(8,128)S(1)} collective-permute-done((f32[1,16,1024]{2,1,0:T(8,128)S(1)}, f32[1,16,1024]{2,1,0:T(8,128)S(1)}, u32[]{:S(2)}, u32[]{:S(2)}) %collective-permute-start) | collective-permute-done | bytes 65568 | tf_op jit(solution)/shard_map/ppermute | solution.py:89
  81.9 0.0 collective-permute-done.1
  81.9 1.0 pad_maximum_fusion
  82.9 1.8 %collective-permute-start.3 = (f32[11,2,1024]{2,1,0:T(2,128)S(1)}, f32[11,2,1024]{2,1,0:T(2,128)S(1)}, u32[]{:S(2)}, u32[]{:S(2)}) collective-permute-start(f32[11,2,1024]{2,1,0:T(2,128)S(1)} %pad_maximum_fusion), channel_id=1, source_target_pairs={{1,0},{2,1},{3,2},{0,3},{5,4},{6,5},{7,6},{4,7},{9,8},{10,9},{11,1... | collective-permute-start | bytes 270344 | tf_op jit(solution)/shard_map/ppermute | solution.py:90
  84.8 0.0 copy-done
  84.8 1.4 %collective-permute-start.2 = (f32[11,1,1024]{2,1,0:T(1,128)S(1)}, f32[11,1,1024]{2,1,0:T(1,128)S(1)}, u32[]{:S(2)}, u32[]{:S(2)}) collective-permute-start(f32[11,1,1024]{2,1,0:T(1,128)S(1)} %pad_maximum_fusion.2), channel_id=1, source_target_pairs={{0,1},{1,2},{2,3},{3,0},{4,5},{5,6},{6,7},{7,4},{8,9},{9,10},{10,1... | collective-permute-start | bytes 135176 | tf_op jit(solution)/shard_map/ppermute | solution.py:89
  86.2 1.1 %collective-permute-done.2 = f32[11,1,1024]{2,1,0:T(1,128)S(1)} collective-permute-done((f32[11,1,1024]{2,1,0:T(1,128)S(1)}, f32[11,1,1024]{2,1,0:T(1,128)S(1)}, u32[]{:S(2)}, u32[]{:S(2)}) %collective-permute-start.2) | collective-permute-done | bytes 45088 | tf_op jit(solution)/shard_map/ppermute | solution.py:89
  87.4 1.4 %collective-permute-done.3 = f32[11,2,1024]{2,1,0:T(2,128)S(1)} collective-permute-done((f32[11,2,1024]{2,1,0:T(2,128)S(1)}, f32[11,2,1024]{2,1,0:T(2,128)S(1)}, u32[]{:S(2)}, u32[]{:S(2)}) %collective-permute-start.3) | collective-permute-done | bytes 90144 | tf_op jit(solution)/shard_map/ppermute | solution.py:90
  88.7 1.2 %select_maximum_fusion.x_ref = f32[11,24,1024]{2,1,0:T(8,128)} fusion(f32[11,2,1024]{2,1,0:T(2,128)S(1)} %collective-permute-done.3, f32[11,1,1024]{2,1,0:T(1,128)S(1)} %collective-permute-done.2, f32[2,16,1024]{2,1,0:T(8,128)S(1)} %collective-permute-done.1, f32[8,16,1024]{2,1,0:T(8,128)S(1)} %bitcast.11, f32[1,16,1024]{2,1,0:T(8,128)S(1)} %collective-permute-done), kind=kLoop, calls=%fused_computation | loop fusion | flops 2703360 | bytes 1937408 | tf_op jit(solution)/shard_map/concatenate | solution.py:91
  89.9 8.2 %shard_map.177 = f32[16,32,2048]{2,1,0:T(8,128)} custom-call(f32[11,24,1024]{2,1,0:T(8,128)} %select_maximum_fusion.x_ref, bf16[64,96]{1,0:T(8,128)(2,1)} %constant.49.clone.r_ref, bf16[384,256]{1,0:T(8,128)(2,1)} %constant.50.clone.t_ref), custom_call_target="tpu_custom_call" | custom-call | tf_op jit(solution)/shard_map/pallas_call | solution.py:334
  (1 shorter events, 0.0 us)
Async XLA Ops:
  67.3 17.5 %copy-start = (f32[128,1024]{1,0:T(8,128)S(1)}, f32[128,1024]{1,0:T(8,128)}, u32[]{:S(2)}) copy-start(f32[128,1024]{1,0:T(8,128)} %shard_map.176) | copy-start | bytes 1572868
  68.3 13.7 %collective-permute-start.1 = (f32[2,16,1024]{2,1,0:T(8,128)S(1)}, f32[2,16,1024]{2,1,0:T(8,128)S(1)}, u32[]{:S(2)}, u32[]{:S(2)}) collective-permute-start(f32[2,16,1024]{2,1,0:T(8,128)S(1)} %bitcast.16), channel_id=1, source_target_pairs={{4,0},{8,4},{12,8},{16,12},{20,16},{24,20},{28,24},{0,28},{5,1},{9... | collective-permute-start | bytes 393224 | tf_op jit(solution)/shard_map/ppermute | solution.py:90
  76.1 5.8 %collective-permute-start = (f32[1,16,1024]{2,1,0:T(8,128)S(1)}, f32[1,16,1024]{2,1,0:T(8,128)S(1)}, u32[]{:S(2)}, u32[]{:S(2)}) collective-permute-start(f32[1,16,1024]{2,1,0:T(8,128)S(1)} %slice_bitcast_fusion), channel_id=1, source_target_pairs={{0,4},{4,8},{8,12},{12,16},{16,20},{20,24},{24,28},{28,0},{1,5},{5... | collective-permute-start | bytes 196616 | tf_op jit(solution)/shard_map/ppermute | solution.py:89
  82.9 5.8 %collective-permute-start.3 = (f32[11,2,1024]{2,1,0:T(2,128)S(1)}, f32[11,2,1024]{2,1,0:T(2,128)S(1)}, u32[]{:S(2)}, u32[]{:S(2)}) collective-permute-start(f32[11,2,1024]{2,1,0:T(2,128)S(1)} %pad_maximum_fusion), channel_id=1, source_target_pairs={{1,0},{2,1},{3,2},{0,3},{5,4},{6,5},{7,6},{4,7},{9,8},{10,9},{11,1... | collective-permute-start | bytes 270344 | tf_op jit(solution)/shard_map/ppermute | solution.py:90
  84.8 2.6 %collective-permute-start.2 = (f32[11,1,1024]{2,1,0:T(1,128)S(1)}, f32[11,1,1024]{2,1,0:T(1,128)S(1)}, u32[]{:S(2)}, u32[]{:S(2)}) collective-permute-start(f32[11,1,1024]{2,1,0:T(1,128)S(1)} %pad_maximum_fusion.2), channel_id=1, source_target_pairs={{0,1},{1,2},{2,3},{3,0},{4,5},{5,6},{6,7},{7,4},{8,9},{9,10},{10,1... | collective-permute-start | bytes 135176 | tf_op jit(solution)/shard_map/ppermute | solution.py:89

commit v2 on v1

--- a/solution.py
+++ b/solution.py
@@ -181,75 +181,112 @@
     return mul(a, d, dims) + mul(b, c, dims) + mul(a, c, dims)
 
 
-def call(body, out_shape, *operands):
-    return pl.pallas_call(
-        body,
-        out_shape=jax.ShapeDtypeStruct(out_shape, jnp.float32),
-        in_specs=[pl.BlockSpec(memory_space=pltpu.VMEM)] * len(operands),
-        out_specs=pl.BlockSpec(memory_space=pltpu.VMEM),
-        compiler_params=pltpu.CompilerParams(vmem_limit_bytes=60 * 1024 * 1024),
-    )(*operands)
-
-
-def exchange_kernel(blocks_z, blocks_y, x_ref, o_ref, send_sem, recv_sem, own_sem):
+def exchange(blocks_z, blocks_y, x_ref, o_ref, send_sem, recv_sem, own_sem):
     devices = blocks_z * blocks_y
     me = lax.axis_index("gz") * blocks_y + lax.axis_index("gy")
-
-    def partner(step):
+    copies = []
+    for step in sorted(range(1, devices), key=lambda s: abs(s - devices // 2)):
         other = lax.rem(me + step, devices)
-        return other, (other // blocks_y, lax.rem(other, blocks_y))
-
-    barrier = pltpu.get_barrier_semaphore()
-    for step in range(1, devices):
-        pl.semaphore_signal(barrier, inc=1, device_id=partner(step)[1], device_id_type=MESH)
-    own = pltpu.make_async_copy(x_ref.at[me], o_ref.at[me], own_sem)
-    own.start()
-    pl.semaphore_wait(barrier, devices - 1)
-    copies = []
-    for step in range(1, devices):
-        other, place = partner(step)
         copy = pltpu.make_async_remote_copy(
             src_ref=x_ref.at[other], dst_ref=o_ref.at[me],
             send_sem=send_sem.at[step], recv_sem=recv_sem.at[step],
-            device_id=place, device_id_type=MESH,
+            device_id=(other // blocks_y, lax.rem(other, blocks_y)), device_id_type=MESH,
         )
         copy.start()
         copies.append(copy)
+    own = pltpu.make_async_copy(x_ref.at[me], o_ref.at[me], own_sem)
+    own.start()
+    copies.append(own)
+    return copies
+
+
+def remote(source, target, sems, number, place):
+    copy = pltpu.make_async_remote_copy(
+        src_ref=source, dst_ref=target, send_sem=sems.at[0, number], recv_sem=sems.at[1, number],
+        device_id=place, device_id_type=MESH,
+    )
+    copy.start()
+    return copy
+
+
+def main_kernel(sizes, *refs):
+    columns, count, blocks_z, blocks_y, n_tables = sizes
+    devices = blocks_z * blocks_y
+    q_ref, k_ref = refs[0], refs[1]
+    sources = refs[2 : 2 + n_tables]
+    out = refs[2 + n_tables]
+    tables = refs[3 + n_tables : 3 + 2 * n_tables]
+    (sent, held, back, home, coarse, up, down, from_low, from_high,
+     table_sem, send_a, recv_a, send_b, recv_b, own_sem, halo_sem) = refs[3 + 2 * n_tables :]
+    loads = [pltpu.make_async_copy(s, t, table_sem.at[i]) for i, (s, t) in enumerate(zip(sources, tables))]
+    for load in loads:
+        load.start()
+    gz, gy = lax.axis_index("gz"), lax.axis_index("gy")
+    me = gz * blocks_y + gy
+    barrier = pltpu.get_barrier_semaphore()
+    for step in range(1, devices):
+        other = lax.rem(me + step, devices)
+        pl.semaphore_signal(
+            barrier, inc=1, device_id=(other // blocks_y, lax.rem(other, blocks_y)), device_id_type=MESH
+        )
+    for load in loads[:4]:
+        load.wait()
+    table_x = (tables[0][...], tables[1][...])
+    first_stage(2 * columns, q_ref, k_ref, table_x, (tables[2][...], tables[3][...]), sent)
+    pl.semaphore_wait(barrier, devices - 1)
+    copies = exchange(blocks_z, blocks_y, sent, held, send_a, recv_a, own_sem.at[0])
+    for load in loads[4:]:
+        load.wait()
     for copy in copies:
         copy.wait()
-    own.wait()
-
-
-def exchange(blocks, blocks_z, blocks_y, number):
-    devices = blocks_z * blocks_y
-    return pl.pallas_call(
-        functools.partial(exchange_kernel, blocks_z, blocks_y),
-        out_shape=jax.ShapeDtypeStruct(blocks.shape, blocks.dtype),
-        in_specs=[pl.BlockSpec(memory_space=pltpu.VMEM)],
-        out_specs=pl.BlockSpec(memory_space=pltpu.VMEM),
-        scratch_shapes=[
-            pltpu.SemaphoreType.DMA((devices,)),
-            pltpu.SemaphoreType.DMA((devices,)),
-            pltpu.SemaphoreType.DMA,
-        ],
-        compiler_params=pltpu.CompilerParams(collective_id=number, has_side_effects=True),
-    )(blocks)
-
-
-def first_kernel(width, q_ref, k_ref, wh, wl, kh, kl, o_ref):
+    pairs = [(tables[i][...], tables[i + 1][...]) for i in range(4, n_tables, 2)]
+    middle_stage(columns, count, blocks_z, blocks_y, held, pairs, back)
+    copies = exchange(blocks_z, blocks_y, back, home, send_b, recv_b, own_sem.at[1])
+    for copy in copies:
+        copy.wait()
+    planes, rows, width = coarse.shape
+    turned = jnp.transpose(home[...].reshape(width, LANES))
+    made = mul3(split(turned), (tables[0][...], tables[1][...])).reshape(planes, rows, width)
+    coarse[...] = made
+    above = (lax.rem(gz + 1, blocks_z), gy)
+    below = (lax.rem(gz + blocks_z - 1, blocks_z), gy)
+    copies = [
+        remote(coarse.at[pl.ds(planes - 1, 1)], out.at[pl.ds(0, 1), pl.ds(0, rows)], halo_sem, 0, above),
+        remote(coarse.at[pl.ds(0, 2)], out.at[pl.ds(planes + 1, 2), pl.ds(0, rows)], halo_sem, 1, below),
+    ]
+    out[1 : planes + 1, :rows, :] = made
+    for p in range(1, planes + 1):
+        up[p : p + 1, :] = coarse[p - 1, rows - 1 : rows, :]
+        down[2 * p : 2 * p + 2, :] = coarse[p - 1, 0:2, :]
+    for copy in copies:
+        copy.wait()
+    for p in (0, planes + 1, planes + 2):
+        up[p : p + 1, :] = out[p, rows - 1 : rows, :]
+        down[2 * p : 2 * p + 2, :] = out[p, 0:2, :]
+    above = (gz, lax.rem(gy + 1, blocks_y))
+    below = (gz, lax.rem(gy + blocks_y - 1, blocks_y))
+    copies = [remote(up, from_low, halo_sem, 2, above), remote(down, from_high, halo_sem, 3, below)]
+    for copy in copies:
+        copy.wait()
+    empty = jnp.zeros((5, width), jnp.float32)
+    for p in range(planes + 3):
+        rim = [from_low[p : p + 1, :], from_high[2 * p : 2 * p + 2, :], empty]
+        out[p, rows : rows + 8, :] = jnp.concatenate(rim, axis=0)
+
+
+def first_stage(width, q_ref, k_ref, table_x, lines_x, o_ref):
     devices = o_ref.shape[0]
     dims = ((1,), (1,))
-    sent = mul3((wh[...], wl[...]), split(q_ref[...]), dims)
+    sent = mul3(lines_x, split(k_ref[...]), dims)
+    o_ref[:, width:, :] = sent.reshape(devices, 8, LANES)
+    sent = mul3(table_x, split(q_ref[...]), dims)
     o_ref[:, :width, :] = sent.reshape(devices, width, LANES)
-    sent = mul3((kh[...], kl[...]), split(k_ref[...]), dims)
-    o_ref[:, width:, :] = sent.reshape(devices, 8, LANES)
-
-
-def middle_kernel(columns, count, x_ref, yh, yl, ch, cl, sh, sl, ah, al, bh, bl, o_ref):
-    blocks_z, blocks_y = o_ref.shape[0], o_ref.shape[1]
+
+
+def middle_stage(columns, count, blocks_z, blocks_y, held, tables, o_ref):
     planes = count // blocks_z
-    table_y = (yh[...], yl[...])
-    cos_z, sin_z = (ch[...], cl[...]), (sh[...], sl[...])
+    table_y, cos_z, sin_z, green_a, green_b = tables
+    x_ref = held[...].reshape(blocks_z, blocks_y, *held.shape[1:])
     lane = lax.broadcasted_iota(jnp.int32, (1, LANES), 1)
     sign = jnp.where(lane < count, 1.0, -1.0)
 
@@ -272,11 +309,11 @@
     )
     data = lines_first(mul3(split(data), table_y))
     deep = blocks_y * LANES
-    green = lines_first(mul3(split(green), (yh[:deep, :], yl[:deep, :])))
+    green = lines_first(mul3(split(green), tuple(t[:deep, :] for t in table_y)))
     data = split(data)
     data = mul3(cos_z, data) + sign * swap(mul3(sin_z, data))
     green = split(green)
-    green = mul3((ah[...], al[...]), green) - sign * swap(mul3((bh[...], bl[...]), green))
+    green = mul3(green_a, green) - sign * swap(mul3(green_b, green))
     other = swap(green)
     real = jnp.where(lane < count, green, other)
     imag = jnp.where(lane < count, -other, green)
@@ -286,16 +323,14 @@
     data = jnp.concatenate([data[p * size : (p + 1) * size, :] for p in range(planes)], axis=1)
     data = mul3(split(data), table_y, ((1,), (1,)))
     for c in range(2):
-        for y in range(blocks_y):
-            start = (c * blocks_y + y) * LANES
-            o_ref[:, y, c * columns : (c + 1) * columns, :] = data[:, start : start + LANES].reshape(
-                blocks_z, columns, LANES
+        pieces = [
+            data[:, (c * blocks_y + y) * LANES : (c * blocks_y + y + 1) * LANES].reshape(
+                blocks_z, 1, columns, LANES
             )
-
-
-def last_kernel(x_ref, wh, wl, o_ref):
-    turned = jnp.transpose(x_ref[...])
-    o_ref[...] = mul3(split(turned), (wh[...], wl[...]))
+            for y in range(blocks_y)
+        ]
+        piece = jnp.concatenate(pieces, axis=1).reshape(blocks_z * blocks_y, columns, LANES)
+        o_ref[:, c * columns : (c + 1) * columns, :] = piece
 
 
 def refine_kernel(x_ref, r_ref, t_ref, o_ref):
@@ -322,11 +357,10 @@
     return made
 
 
-def refine(coarse, planes, rows, width, replicas):
-    haloed = extended(extended(coarse, "gz", 0), "gy", 1)
-    deep = -(-(rows + 3) // 8) * 8
-    haloed = jnp.pad(haloed, ((0, 0), (0, deep - rows - 3), (0, 0)))
-    along_y = np.pad(rim_table(rows), ((0, 0), (0, deep - rows - 3)))
+def refine(haloed, planes, rows, width, replicas):
+    along_y = rim_table(rows)
+    empty = np.zeros((2 * rows, 5))
+    along_y = np.concatenate([along_y[:, 1 : rows + 1], along_y[:, :1], along_y[:, rows + 1 :], empty], axis=1)
     both = jnp.asarray(np.kron(rim_table(1), along_y), jnp.bfloat16)
     count = width // replicas
     spread = refined(np.eye(width).reshape(width, count, replicas), 1).reshape(width, 2 * width)
@@ -366,7 +400,7 @@
     columns = count * half // devices
     lines = max(1, columns // half)
     fits = place == LANES and 2 * count == LANES and columns % 8 == 0 and 2 * lines <= 8
-    if not fits or LANES % replicas or width < 3 * LANES:
+    if not fits or LANES % replicas or width < 3 * LANES or rows % 8 or planes < 2:
         return plain(charges, kernel)
     table_x = table(x_table(count, replicas, devices).reshape(-1, width))
     lines_x = x_kernel_table(count, replicas, devices).reshape(devices, 2 * lines, count)
@@ -378,19 +412,33 @@
     green_a = table(scale * z_green_table(count, planes, columns, half, np.cos, np.sin))
     green_b = table(scale * z_green_table(count, planes, columns, half, lambda t: -np.sin(t), np.cos))
 
-    sent = call(
-        functools.partial(first_kernel, 2 * columns), (devices, 2 * columns + 8, LANES),
-        charges.reshape(place, width), kernel.reshape(place, count), *table_x, *lines_x,
-    )
-    held = exchange(sent, blocks_z, blocks_y, 0)
-    sent = call(
-        functools.partial(middle_kernel, columns, count), (blocks_z, blocks_y, 2 * columns, LANES),
-        held.reshape(blocks_z, blocks_y, 2 * columns + 8, LANES),
-        *table_y, *cos_z, *sin_z, *green_a, *green_b,
-    )
-    held = exchange(sent.reshape(devices, 2 * columns, LANES), blocks_z, blocks_y, 1)
-    coarse = call(last_kernel, (place, width), held.reshape(width, LANES), *table_x)
-    return refine(coarse.reshape(planes, rows, width), planes, rows, width, replicas)
+    tables = [*table_x, *lines_x, *table_y, *cos_z, *sin_z, *green_a, *green_b]
+    size = 2 * columns
+    packed = -(-(planes + 3) // 8) * 8
+    vmem = pl.BlockSpec(memory_space=pltpu.VMEM)
+    block = lambda *shape: pltpu.VMEM(shape, jnp.float32)
+    haloed = pl.pallas_call(
+        functools.partial(main_kernel, (columns, count, blocks_z, blocks_y, len(tables))),
+        out_shape=jax.ShapeDtypeStruct((planes + 3, rows + 8, width), jnp.float32),
+        in_specs=[vmem, vmem] + [pl.BlockSpec(memory_space=pl.ANY)] * len(tables),
+        out_specs=vmem,
+        scratch_shapes=[
+            *(pltpu.VMEM(t.shape, t.dtype) for t in tables),
+            block(devices, size + 8, LANES), block(devices, size + 8, LANES),
+            block(devices, size, LANES), block(devices, size, LANES),
+            block(planes, rows, width),
+            block(packed, width), block(2 * packed, width),
+            block(packed, width), block(2 * packed, width),
+            pltpu.SemaphoreType.DMA((len(tables),)),
+            *(pltpu.SemaphoreType.DMA((devices,)) for _ in range(4)),
+            pltpu.SemaphoreType.DMA((2,)),
+            pltpu.SemaphoreType.DMA((2, 4)),
+        ],
+        compiler_params=pltpu.CompilerParams(
+            collective_id=0, has_side_effects=True, vmem_limit_bytes=60 * 1024 * 1024
+        ),
+    )(charges.reshape(place, width), kernel.reshape(place, count), *tables)
+    return refine(haloed, planes, rows, width, replicas)
 
 
 def solution(mesh):

time: 98.6 us -> 71.3 us (0.72)
  starting transfers between devices: 10.3 us -> 0 us
  waiting for transfers between devices: 8.3 us -> 0 us
  Pallas kernels: 75.5 us -> 71.1 us
  other arithmetic: 2.24 us -> 0 us
  local copies, waits for them, and re-layouts: 1.83 us -> 0 us
    ppermute x4 -> x0, starting transfers between devices: 10.3 us -> none  [the longest x2 8.83 us: extended(): high = lax.ppermute(lax.slice_in_dim(block, 0, 2, axis=dim), axis, backward)]
    ppermute x4 -> x0, waiting for transfers between devices: 8.3 us -> none  [the longest x2 6.95 us: extended(): lax.ppermute(lax.slice_in_dim(block, block.shape[dim] - 1, None, axis=dim...]
    pallas_call x5 -> x1, Pallas kernels: 67.3 us -> 62.9 us  [per_device(): pl.pallas_call(functools.partial(main_kernel, (columns, count, blocks_z,...]
    concatenate x2 -> x0, other arithmetic: 2.2 us -> none  [extended(): return jnp.concatenate([low, block, high], axis=dim)]
    slice x2 -> x0, local copies, waits for them, and re-layouts: 1.83 us -> none  [the longest x1 0.99 us: extended(): high = lax.ppermute(lax.slice_in_dim(block, 0, 2, axis=dim), axis, backward)]
  transfers between devices with their start and end apart: 4 -> 0, of which waited for: 3 -> 0; matrix products, arithmetic and copies ran while one was open for 1% -> 0% of each run, Pallas kernels for 0% -> 0%
where the time goes in v2:
time: 71.3 us; the launch traced here: 71.2 us
  Pallas kernels  71.1 us (100%)
    pallas_call x1, Pallas kernels, per_device(): pl.pallas_call(functools.partial(main_kernel, (columns, count, blocks_z,...  62.9 us
    pallas_call x1, Pallas kernels, refine(): pl.pallas_call(refine_kernel, grid=(planes,), out_shape=jax.ShapeDtypeStr...  8.24 us

profile of v2, /device:TPU:1, one launch (start us, length us, event | category | flops | bytes accessed | tf_op | source)
XLA Modules:
  0.0 71.2 jit_solution(12090015538300759517)
XLA Ops:
  0.0 62.9 %shard_map.172.x_ref = f32[11,24,1024]{2,1,0:T(8,128)} custom-call(f32[128,1024]{1,0:T(8,128)} %bitcast.2, f32[128,64]{1,0:T(8,128)} %bitcast.3, bf16[1024,1024]{1,0:T(8,128)(2,1)} %constant.32.clone.refs_2_, bf16[1024,1024]{1,0:T(8,128)(2,1)} %constant.33.clone.refs_3_, bf16[256,64]{1,0:T(8,128)(2,1)} %constant.34.clone.refs_4_, ...), custom_call_target="tpu_custom_call" | custom-call | tf_op jit(solution)/shard_map/pallas_call | solution.py:420
  62.9 8.2 %shard_map.173 = f32[16,32,2048]{2,1,0:T(8,128)} custom-call(f32[11,24,1024]{2,1,0:T(8,128)} %shard_map.172.x_ref, bf16[64,96]{1,0:T(8,128)(2,1)} %constant.46.clone.r_ref, bf16[384,256]{1,0:T(8,128)(2,1)} %constant.47.clone.t_ref), custom_call_target="tpu_custom_call" | custom-call | tf_op jit(solution)/shard_map/pallas_call | solution.py:368

commit v3 on v2

--- a/solution.py
+++ b/solution.py
@@ -181,22 +181,28 @@
     return mul(a, d, dims) + mul(b, c, dims) + mul(a, c, dims)
 
 
-def exchange(blocks_z, blocks_y, x_ref, o_ref, send_sem, recv_sem, own_sem):
-    devices = blocks_z * blocks_y
+GROUPS = 4
+ORDER = (2, 3, 1, 0)
+
+
+def send_group(blocks_z, blocks_y, offset, x_ref, o_ref, sems, own_sem):
+    size = blocks_z * blocks_y // GROUPS
     me = lax.axis_index("gz") * blocks_y + lax.axis_index("gy")
+    target = lax.rem(me // size + offset, GROUPS)
     copies = []
-    for step in sorted(range(1, devices), key=lambda s: abs(s - devices // 2)):
-        other = lax.rem(me + step, devices)
-        copy = pltpu.make_async_remote_copy(
-            src_ref=x_ref.at[other], dst_ref=o_ref.at[me],
-            send_sem=send_sem.at[step], recv_sem=recv_sem.at[step],
-            device_id=(other // blocks_y, lax.rem(other, blocks_y)), device_id_type=MESH,
-        )
+    for step in range(size):
+        if offset == 0 and step == 0:
+            copy = pltpu.make_async_copy(x_ref.at[me], o_ref.at[me], own_sem)
+        else:
+            other = target * size + lax.rem(lax.rem(me, size) + step, size)
+            number = offset * size + step
+            copy = pltpu.make_async_remote_copy(
+                src_ref=x_ref.at[other], dst_ref=o_ref.at[me],
+                send_sem=sems[0].at[number], recv_sem=sems[1].at[number],
+                device_id=(other // blocks_y, lax.rem(other, blocks_y)), device_id_type=MESH,
+            )
         copy.start()
         copies.append(copy)
-    own = pltpu.make_async_copy(x_ref.at[me], o_ref.at[me], own_sem)
-    own.start()
-    copies.append(own)
     return copies
 
 
@@ -231,22 +237,44 @@
         )
     for load in loads[:4]:
         load.wait()
-    table_x = (tables[0][...], tables[1][...])
-    first_stage(2 * columns, q_ref, k_ref, table_x, (tables[2][...], tables[3][...]), sent)
-    pl.semaphore_wait(barrier, devices - 1)
-    copies = exchange(blocks_z, blocks_y, sent, held, send_a, recv_a, own_sem.at[0])
+    width = q_ref.shape[1]
+    size = devices // GROUPS
+    deep = size * 2 * columns
+    green = mul3((tables[2][...], tables[3][...]), split(k_ref[...]), ((1,), (1,)))
+    sent[:, 2 * columns :, :] = green.reshape(devices, 8, LANES)
+    charges = split(q_ref[...])
+
+    def table_rows(group):
+        place = pl.ds(pl.multiple_of(group * deep, deep), deep)
+        return tables[0][place, :], tables[1][place, :]
+
+    copies = []
+    for offset in ORDER:
+        group = lax.rem(me // size + offset, GROUPS)
+        made = mul3(table_rows(group), charges, ((1,), (1,)))
+        sent[pl.ds(group * size, size), : 2 * columns, :] = made.reshape(size, 2 * columns, LANES)
+        if not copies:
+            pl.semaphore_wait(barrier, devices - 1)
+        copies += send_group(blocks_z, blocks_y, offset, sent, held, (send_a, recv_a), own_sem.at[0])
     for load in loads[4:]:
         load.wait()
     for copy in copies:
         copy.wait()
     pairs = [(tables[i][...], tables[i + 1][...]) for i in range(4, n_tables, 2)]
     middle_stage(columns, count, blocks_z, blocks_y, held, pairs, back)
-    copies = exchange(blocks_z, blocks_y, back, home, send_b, recv_b, own_sem.at[1])
-    for copy in copies:
-        copy.wait()
-    planes, rows, width = coarse.shape
-    turned = jnp.transpose(home[...].reshape(width, LANES))
-    made = mul3(split(turned), (tables[0][...], tables[1][...])).reshape(planes, rows, width)
+    copies = [
+        send_group(blocks_z, blocks_y, offset, back, home, (send_b, recv_b), own_sem.at[1])
+        for offset in ORDER
+    ]
+    planes, rows, _ = coarse.shape
+    made = jnp.zeros((LANES, width), jnp.float32)
+    for offset, group_copies in zip(ORDER, copies):
+        for copy in group_copies:
+            copy.wait()
+        group = lax.rem(me // size + GROUPS - offset, GROUPS)
+        turned = jnp.transpose(home[pl.ds(group * size, size)].reshape(deep, LANES))
+        made += mul3(split(turned), table_rows(group))
+    made = made.reshape(planes, rows, width)
     coarse[...] = made
     above = (lax.rem(gz + 1, blocks_z), gy)
     below = (lax.rem(gz + blocks_z - 1, blocks_z), gy)
@@ -274,15 +302,6 @@
         out[p, rows : rows + 8, :] = jnp.concatenate(rim, axis=0)
 
 
-def first_stage(width, q_ref, k_ref, table_x, lines_x, o_ref):
-    devices = o_ref.shape[0]
-    dims = ((1,), (1,))
-    sent = mul3(lines_x, split(k_ref[...]), dims)
-    o_ref[:, width:, :] = sent.reshape(devices, 8, LANES)
-    sent = mul3(table_x, split(q_ref[...]), dims)
-    o_ref[:, :width, :] = sent.reshape(devices, width, LANES)
-
-
 def middle_stage(columns, count, blocks_z, blocks_y, held, tables, o_ref):
     planes = count // blocks_z
     table_y, cos_z, sin_z, green_a, green_b = tables
@@ -310,15 +329,27 @@
     data = lines_first(mul3(split(data), table_y))
     deep = blocks_y * LANES
     green = lines_first(mul3(split(green), tuple(t[:deep, :] for t in table_y)))
-    data = split(data)
-    data = mul3(cos_z, data) + sign * swap(mul3(sin_z, data))
     green = split(green)
     green = mul3(green_a, green) - sign * swap(mul3(green_b, green))
-    other = swap(green)
-    real = jnp.where(lane < count, green, other)
-    imag = jnp.where(lane < count, -other, green)
-    data = split(data * real + swap(data) * imag)
-    data = mul3(cos_z, data) - sign * swap(mul3(sin_z, data))
+    half = cos_z[0].shape[0] // count
+
+    def parts(values):
+        values = values.reshape(count, columns, LANES)
+        return [
+            values[:, m : m + half, :].reshape(count * half, LANES) for m in range(0, columns, half)
+        ]
+
+    made = []
+    for part, factor in zip(parts(data), parts(green)):
+        part = split(part)
+        part = mul3(cos_z, part) + sign * swap(mul3(sin_z, part))
+        other = swap(factor)
+        real = jnp.where(lane < count, factor, other)
+        imag = jnp.where(lane < count, -other, factor)
+        part = split(part * real + swap(part) * imag)
+        part = mul3(cos_z, part) - sign * swap(mul3(sin_z, part))
+        made.append(part.reshape(count, half, LANES))
+    data = jnp.concatenate(made, axis=1).reshape(count * columns, LANES)
     size = blocks_z * columns
     data = jnp.concatenate([data[p * size : (p + 1) * size, :] for p in range(planes)], axis=1)
     data = mul3(split(data), table_y, ((1,), (1,)))
@@ -340,13 +371,17 @@
     fine = mul(r_ref[...], low) + mul(r_ref[...], high)
     high, low = split(fine)
     blocks = fine.shape[1] // LANES
+    def windows(values):
+        made = []
+        for b in range(blocks):
+            pieces = [(b + s) % blocks * LANES for s in (-1, 0, 1)]
+            made.append(jnp.concatenate([values[:, p : p + LANES] for p in pieces], axis=1))
+        return jnp.concatenate(made, axis=0)
+
+    made = mul(windows(low), t_ref[...]) + mul(windows(high), t_ref[...])
     for b in range(blocks):
-        def window(values):
-            pieces = [(b + s) % blocks * LANES for s in (-1, 0, 1)]
-            return jnp.concatenate([values[:, p : p + LANES] for p in pieces], axis=1)
-
-        made = mul(window(low), t_ref[...]) + mul(window(high), t_ref[...])
-        o_ref[:, :, 2 * b * LANES : 2 * (b + 1) * LANES] = made.reshape(2, -1, 2 * LANES)
+        piece = made[b * fine.shape[0] : (b + 1) * fine.shape[0], :]
+        o_ref[:, :, 2 * b * LANES : 2 * (b + 1) * LANES] = piece.reshape(2, -1, 2 * LANES)
 
 
 def rim_table(count):
@@ -400,14 +435,15 @@
     columns = count * half // devices
     lines = max(1, columns // half)
     fits = place == LANES and 2 * count == LANES and columns % 8 == 0 and 2 * lines <= 8
-    if not fits or LANES % replicas or width < 3 * LANES or rows % 8 or planes < 2:
+    if not fits or LANES % replicas or width < 3 * LANES or rows % 8 or planes < 2 \
+            or devices % GROUPS or half % 8 or columns % half:
         return plain(charges, kernel)
     table_x = table(x_table(count, replicas, devices).reshape(-1, width))
     lines_x = x_kernel_table(count, replicas, devices).reshape(devices, 2 * lines, count)
     lines_x = table(np.pad(lines_x, ((0, 0), (0, 8 - 2 * lines), (0, 0))).reshape(devices * 8, count))
     table_y = table(y_table(count, planes, rows))
-    cos_z = table(z_table(count, planes, columns, columns, 1, np.cos))
-    sin_z = table(z_table(count, planes, columns, columns, 1, np.sin))
+    cos_z = table(z_table(count, planes, half, half, 1, np.cos))
+    sin_z = table(z_table(count, planes, half, half, 1, np.sin))
     scale = 1.0 / count**3
     green_a = table(scale * z_green_table(count, planes, columns, half, np.cos, np.sin))
     green_b = table(scale * z_green_table(count, planes, columns, half, lambda t: -np.sin(t), np.cos))

time: 71.3 us -> 65.8 us (0.923)
  Pallas kernels: 71.1 us -> 65.6 us
    pallas_call x1, Pallas kernels: 62.9 us -> 58.2 us  [per_device(): pl.pallas_call(functools.partial(main_kernel, (columns, count, blocks_z,...]
    pallas_call x1, Pallas kernels: 8.24 us -> 7.47 us  [refine(): pl.pallas_call(refine_kernel, grid=(planes,), out_shape=jax.ShapeDtypeStr...]
where the time goes in v3:
time: 65.8 us; the launch traced here: 65.6 us
  Pallas kernels  65.6 us (100%)
    pallas_call x1, Pallas kernels, per_device(): pl.pallas_call(functools.partial(main_kernel, (columns, count, blocks_z,...  58.2 us
    pallas_call x1, Pallas kernels, refine(): pl.pallas_call(refine_kernel, grid=(planes,), out_shape=jax.ShapeDtypeStr...  7.47 us

profile of v3, /device:TPU:1, one launch (start us, length us, event | category | flops | bytes accessed | tf_op | source)
XLA Modules:
  0.0 65.6 jit_solution(16117222451116883876)
XLA Ops:
  0.0 58.2 %shard_map.172.x_ref = f32[11,24,1024]{2,1,0:T(8,128)} custom-call(f32[128,1024]{1,0:T(8,128)} %bitcast.2, f32[128,64]{1,0:T(8,128)} %bitcast.3, bf16[1024,1024]{1,0:T(8,128)(2,1)} %constant.32.clone.refs_2_, bf16[1024,1024]{1,0:T(8,128)(2,1)} %constant.33.clone.refs_3_, bf16[256,64]{1,0:T(8,128)(2,1)} %constant.34.clone.refs_4_, ...), custom_call_target="tpu_custom_call" | custom-call | tf_op jit(solution)/shard_map/pallas_call | solution.py:456
  58.2 7.5 %shard_map.173 = f32[16,32,2048]{2,1,0:T(8,128)} custom-call(f32[11,24,1024]{2,1,0:T(8,128)} %shard_map.172.x_ref, bf16[64,96]{1,0:T(8,128)(2,1)} %constant.46.clone.r_ref, bf16[384,256]{1,0:T(8,128)(2,1)} %constant.47.clone.t_ref), custom_call_target="tpu_custom_call" | custom-call | tf_op jit(solution)/shard_map/pallas_call | solution.py:403
